TPU v7x, 128 devices: a whole 4x4x4 slice. The times are simulated.
128 devices in a mesh: gx: 8 (over z, core), wa: 16 (over x, y).
Axes of the slice: x: 4, y: 4, z: 4, core: 2. Of those that a mesh axis runs over, the one named last changes fastest.
Arguments:
- positions: float32 [2048, 3, 256], P(('gx', 'wa')), may hold values from 0 to 1
- weights: float32 [2048, 256], P(('gx', 'wa')), may hold values from 0.5 to 2
- block_count: int32 [2048], P(('gx', 'wa')), may hold values from 1 to 256
- send_list: int32 [128, 16, 2], P(('gx', 'wa')), may hold values from 0 to 15
- unit_pair: int32 [128, 32], P(('gx', 'wa')), may hold values from 0 to 31, each once within a row
- unit_live: int32 [128], P(('gx', 'wa')), may hold values from 4 to 32, as said below
Outputs:
- slab_counts: float32 [8, 30, 20], P('gx')
- totals: float32 [30, 20], replicated
Inputs may be any that keep to these rules, and one draw needn't show every extreme that they name: `unit_pair`: each row holds every slot number once. `unit_live`: the active units of a device are the first ones of its list; some device has all 32 active.
All inputs are finite; a program needn't handle non-finite values.
Results may differ from a plain program's by a relative error of at most 0.0003.
Values sent between devices are 32-bit elements; how exact they have to be, the bound alone decides.
A program may use at most 64 MiB of HBM per device.

v0:
```python
import functools

import jax
import jax.numpy as jnp
from jax import lax
from jax.experimental import pallas as pl
from jax.experimental.pallas import tpu as pltpu
from jax.sharding import PartitionSpec as P

SBINS = 30
MUBINS = 20
HS, HM = SBINS // 2, MUBINS // 2
reach = 0.5
viewer = (0.5, 0.5, -1.5)
TILES = 48
f32, bf16, i32 = jnp.float32, jnp.bfloat16, jnp.int32
MESH = pl.DeviceIdType.MESH


def hats(at, first, second, half):
    spot = jnp.concatenate([at, at - half], axis=0).astype(bf16)
    first = jnp.concatenate([first, first], axis=0).astype(bf16)
    second = jnp.concatenate([second, second], axis=0).astype(bf16)
    zero = jnp.zeros_like(first)
    before = spot == jnp.asarray(-1, bf16)
    out = []
    for q in range(half):
        here = spot == jnp.asarray(q, bf16)
        out.append(jnp.where(here, first, jnp.where(before, second, zero)))
        before = here
    return out


def lane_pick(x, lane):
    numbers = lax.GatherDimensionNumbers(
        offset_dims=(), collapsed_slice_dims=(1,), start_index_map=(1,), operand_batching_dims=(0,), start_indices_batching_dims=(0,)
    )
    return lax.gather(x, lane[..., None], numbers, slice_sizes=(1, 1), mode=lax.GatherScatterMode.PROMISE_IN_BOUNDS)


def tile_terms(cols, lane_at, row):
    def of_a(c):
        return lane_pick(cols, jnp.full((8, 128), lane_at + c, i32))

    def of_b(c):
        return jnp.broadcast_to(row[c : c + 1, :], (8, 128))

    dx, dy, dz = (of_a(c) - of_b(c) for c in range(3))
    square = dx * dx + dy * dy + dz * dz
    norm_a, norm_b = of_a(3), of_b(3)
    s = square * lax.rsqrt(jnp.maximum(square, 1e-30)) - 0.5
    s_at = jnp.floor(s)
    mu = (MUBINS / 2) * jnp.abs(norm_a - norm_b) * lax.rsqrt(
        jnp.maximum(square, 1.0) * (norm_a + norm_b - square)
    ) - 0.5
    mu_at = jnp.floor(mu)
    both = of_a(4) * of_b(4)
    upper = (mu - mu_at) * both
    return s_at, s - s_at, mu_at, both - upper, upper


def iota(shape, d):
    return lax.broadcasted_iota(i32, shape, d)


def plan(a_weights, b_weights):
    def live(halves):
        count = sum(jnp.where(w > 0.0, 1.0, 0.0) for w in halves)
        return jnp.broadcast_to(jnp.sum(count, axis=1, keepdims=True), count.shape)

    n_a, n_b = live(a_weights), live(b_weights)
    rows_a, rows_b = jnp.ceil(n_a / 8), jnp.ceil(n_b / 8)
    lanes_a, lanes_b = jnp.ceil(n_a / 128), jnp.ceil(n_b / 128)
    turned = jnp.where(rows_b * lanes_a < rows_a * lanes_b, 1.0, 0.0)
    n_lanes = jnp.where(turned > 0.0, lanes_a, lanes_b)
    return turned, n_lanes, jnp.where(turned > 0.0, rows_b, rows_a) * n_lanes


def slot_copy(src, dst, send_sem, recv_sem, device):
    return pltpu.make_async_remote_copy(
        src_ref=src, dst_ref=dst, send_sem=send_sem, recv_sem=recv_sem, device_id=device, device_id_type=MESH
    )


def exchange_kernel(
    n_gx, n_wa, live_ref, count_hbm, list_hbm, pair_hbm, pos_hbm, wgt_hbm, out_ref,
    count_ref, list_ref, pair_ref, pos_ref, wgt_ref, home_ref, stage_ref, own_ref, below_ref, deal_ref,
    load_sems, send_sems, recv_sems,
):
    g, w = lax.axis_index("gx"), lax.axis_index("wa")
    above, under = lax.rem(g + 1, n_gx), lax.rem(g + n_gx - 1, n_gx)
    units = 2 * n_wa
    pairs = ((count_hbm, count_ref), (list_hbm, list_ref), (pair_hbm, pair_ref), (pos_hbm, pos_ref), (wgt_hbm, wgt_ref))
    loads = [pltpu.make_async_copy(src, dst, load_sems.at[k]) for k, (src, dst) in enumerate(pairs)]
    for load in loads:
        load.start()
    barrier = pltpu.get_barrier_semaphore()
    for o in range(n_wa):
        p = lax.rem(w + o, n_wa)
        pl.semaphore_signal(barrier, inc=1, device_id=(under, p), device_id_type=MESH)
        if o:
            pl.semaphore_signal(barrier, inc=1, device_id=(g, p), device_id_type=MESH)
    for load in loads:
        load.wait()

    for b in range(pos_ref.shape[1]):
        for h in range(2):
            at = slice(128 * h, 128 * (h + 1))
            home_ref[b, 4 * h : 4 * h + 3, :] = pos_ref[:, b, at]
            keep = iota((1, 128), 1) + 128 * h < count_ref[b]
            home_ref[b, 4 * h + 3 : 4 * h + 4, :] = jnp.where(keep, wgt_ref[b : b + 1, at], 0.0)
    for q in range(units):
        stage_ref[q] = home_ref[list_ref[0, q % 2, q // 2]]
    pl.semaphore_wait(barrier, 2 * n_wa - 1)

    def two(ref, p):
        return ref.at[pl.ds(2 * p, 2)]

    for o in range(n_wa):
        p = lax.rem(w + o, n_wa)
        slot_copy(two(stage_ref, p), two(below_ref, w), send_sems.at[0], recv_sems.at[0], (above, p)).start()
        if o:
            slot_copy(two(stage_ref, p), two(own_ref, w), send_sems.at[1], recv_sems.at[1], (g, p)).start()
    own_ref[pl.ds(2 * w, 2)] = stage_ref[pl.ds(2 * w, 2)]
    rest = pl.ds(0, units - 2)
    below_all = slot_copy(stage_ref, below_ref, send_sems.at[0], recv_sems.at[0], (above, w))
    own_all = slot_copy(stage_ref.at[rest], own_ref.at[rest], send_sems.at[1], recv_sems.at[1], (above, w))
    below_all.wait_recv()
    own_all.wait_recv()

    active = iota((units, 128), 0) < live_ref[0]
    partner = jnp.concatenate([below_ref[pair_ref[0, u]] for u in range(units)], axis=0)
    row = iota((8 * units, 128), 0)
    dead = ((row & 3) == 3) & ((row >> 3) >= live_ref[0])
    mine = jnp.where(dead, 0.0, own_ref[...].reshape(8 * units, 128))
    three = partner.reshape(units, 8, 128)
    tiles = plan(
        [jnp.where(active, own_ref[:, c, :], 0.0) for c in (3, 7)], [three[:, c, :] for c in (3, 7)]
    )[2]
    unit = iota((units, 128), 0).astype(f32)
    key = tiles * units + (units - 1 - unit)
    on_lanes = jnp.sum(jnp.where(iota((units, 128), 0) == iota((units, 128), 1), key, 0.0), axis=0, keepdims=True)
    more = (on_lanes > key) & (iota((units, 128), 1) < units)
    rank = jnp.sum(jnp.where(more, 1.0, 0.0), axis=1, keepdims=True)
    place = jnp.where(rank < n_wa, rank, (units - 1 + n_wa) - rank)
    wide = (units, 8 * units)
    target = jnp.sum(
        jnp.where(iota(wide, 0) == (iota(wide, 1) >> 3), 8.0 * place + (iota(wide, 1) & 7).astype(f32), 0.0),
        axis=0, keepdims=True,
    )
    square = (8 * units, 8 * units)
    choice = jnp.where(iota(square, 0).astype(f32) == target, 1.0, 0.0).astype(bf16)
    left = jnp.concatenate([mine, partner], axis=1)
    chosen = None
    for _ in range(3):
        part = left.astype(bf16)
        moved = jnp.dot(choice, part, preferred_element_type=f32)
        chosen = moved if chosen is None else chosen + moved
        left = left - part.astype(f32)
    for i in range(units):
        for k in range(2):
            deal_ref[i % n_wa, 2 * (i // n_wa) + k] = chosen[8 * i : 8 * i + 8, 128 * k : 128 * k + 128]

    for o in range(1, n_wa):
        p = lax.rem(w + o, n_wa)
        slot_copy(
            deal_ref.at[o], out_ref.at[pl.ds(4 * w, 4)], send_sems.at[2], recv_sems.at[2], (g, p)
        ).start()
    out_ref[pl.ds(4 * w, 4)] = deal_ref[0]
    below_all.wait_send()
    own_all.wait_send()
    dealt = slot_copy(
        deal_ref.at[pl.ds(1, n_wa - 1)], out_ref.at[pl.ds(0, 4 * (n_wa - 1))], send_sems.at[2], recv_sems.at[2], (above, w)
    )
    dealt.wait_recv()
    dealt.wait_send()


def dealt_blocks(n_gx, n_wa, positions, weights, block_count, send_list, unit_pair, unit_live):
    smem, vmem, anywhere = (pl.BlockSpec(memory_space=m) for m in (pltpu.SMEM, pltpu.VMEM, pl.ANY))
    units = 2 * n_wa
    return pl.pallas_call(
        functools.partial(exchange_kernel, n_gx, n_wa),
        out_shape=pltpu.VMEM((2 * units, 8, 128), f32),
        in_specs=[smem] + [anywhere] * 5,
        out_specs=vmem,
        scratch_shapes=[
            pltpu.SMEM(block_count.shape, i32),
            pltpu.SMEM(send_list.shape, i32),
            pltpu.SMEM(unit_pair.shape, i32),
            pltpu.VMEM(positions.shape, f32),
            pltpu.VMEM(weights.shape, f32),
            pltpu.VMEM((positions.shape[1], 8, 128), f32),
            pltpu.VMEM((units, 8, 128), f32),
            pltpu.VMEM((units, 8, 128), f32),
            pltpu.VMEM((units, 8, 128), f32),
            pltpu.VMEM((n_wa, 4, 8, 128), f32),
            pltpu.SemaphoreType.DMA((5,)),
            pltpu.SemaphoreType.DMA((3,)),
            pltpu.SemaphoreType.DMA((3,)),
        ],
        compiler_params=pltpu.CompilerParams(collective_id=0, has_side_effects=True),
    )(unit_live, block_count, send_list, unit_pair, positions, weights)


def total_kernel(
    n_gx, n_wa, scale, in_ref, slab_out, whole_out, gx_ref, slab_ref, whole_ref, column_ref, send_sems, recv_sems
):
    g, w = lax.axis_index("gx"), lax.axis_index("wa")
    barrier = pltpu.get_barrier_semaphore()
    wa_peers = [lax.rem(w + o, n_wa) for o in range(1, n_wa)]
    gx_peers = [lax.rem(g + o, n_gx) for o in range(1, n_gx)]
    for p in wa_peers:
        pl.semaphore_signal(barrier, inc=1, device_id=(g, p), device_id_type=MESH)
    for p in gx_peers:
        pl.semaphore_signal(barrier, inc=1, device_id=(p, w), device_id_type=MESH)
    pl.semaphore_wait(barrier, n_wa + n_gx - 2)

    for p in gx_peers:
        slot_copy(in_ref, gx_ref.at[g], send_sems.at[0], recv_sems.at[0], (p, w)).start()
    for p in wa_peers:
        slot_copy(in_ref, slab_ref.at[w], send_sems.at[1], recv_sems.at[1], (g, p)).start()
    gx_ref[g] = in_ref[...]
    slab_ref[w] = in_ref[...]

    def all_of(ref, n, k):
        some = ref.at[pl.ds(0, n - 1)]
        return slot_copy(some, some, send_sems.at[k], recv_sems.at[k], (lax.rem(g + 1, n_gx), w))

    all_of(gx_ref, n_gx, 0).wait_recv()
    column = jnp.sum(gx_ref[...], axis=0)
    column_ref[...] = column
    whole_ref[w] = column

    for p in wa_peers:
        slot_copy(column_ref, whole_ref.at[w], send_sems.at[2], recv_sems.at[2], (g, p)).start()
    all_of(slab_ref, n_wa, 1).wait_recv()
    slab_out[...] = jnp.sum(slab_ref[...], axis=0) * scale
    all_of(gx_ref, n_gx, 0).wait_send()
    all_of(slab_ref, n_wa, 1).wait_send()
    all_of(whole_ref, n_wa, 2).wait_recv()
    whole_out[...] = jnp.sum(whole_ref[...], axis=0) * (scale / n_gx)
    all_of(whole_ref, n_wa, 2).wait_send()


def totals(n_gx, n_wa, scale, packed):
    vmem = pl.BlockSpec(memory_space=pltpu.VMEM)
    return pl.pallas_call(
        functools.partial(total_kernel, n_gx, n_wa, scale),
        out_shape=(pltpu.VMEM((8, 128), f32), pltpu.VMEM((8, 128), f32)),
        in_specs=[vmem],
        out_specs=(vmem, vmem),
        scratch_shapes=[
            pltpu.VMEM((n_gx, 8, 128), f32),
            pltpu.VMEM((n_wa, 8, 128), f32),
            pltpu.VMEM((n_wa, 8, 128), f32),
            pltpu.VMEM((8, 128), f32),
            pltpu.SemaphoreType.DMA((3,)),
            pltpu.SemaphoreType.DMA((3,)),
        ],
        compiler_params=pltpu.CompilerParams(collective_id=1, has_side_effects=True),
    )(packed)


def unpack_kernel(slab_ref, whole_ref, slab_out, whole_out):
    for ref, out in ((slab_ref, slab_out.at[:, 0, :]), (whole_ref, whole_out)):
        packed = ref[...]
        for k in range(3):
            rows = min(8, MUBINS - 8 * k)
            turned = packed if k == 0 else pltpu.roll(packed, 128 - 32 * k, 1)
            out[8 * k : 8 * k + rows, :] = turned[:rows, :SBINS]


def unpacked(slab, whole):
    vmem = pl.BlockSpec(memory_space=pltpu.VMEM)
    return pl.pallas_call(
        unpack_kernel,
        out_shape=(
            jax.ShapeDtypeStruct((MUBINS, 1, SBINS), f32),
            jax.ShapeDtypeStruct((MUBINS, SBINS), f32),
        ),
        in_specs=[vmem, vmem],
        out_specs=(vmem, vmem),
    )(slab, whole)


def count_kernel(units, blocks_ref, out_ref, rows_ref, cols_ref, per_unit_ref, list_ref, list_smem, terms_ref, acc_ref, sem):
    n_blocks = 2 * units
    scale = SBINS / reach
    groups = n_blocks // 16

    def weights_of(s):
        return [blocks_ref[pl.ds(s, units, stride=2), 4 * h + 3, :] for h in range(2)]

    turned, n_lanes, tiles = plan(weights_of(0), weights_of(1))
    low = iota((units, units), 1) < iota((units, units), 0)
    start = jnp.dot(jnp.where(low, 1.0, 0.0), tiles, preferred_element_type=f32)
    unit = iota((units, 128), 0).astype(f32)
    eighth = jnp.floor(unit / 8)
    lane16 = 2.0 * (unit - 8.0 * eighth) + turned
    dummy = jnp.float32(2 * n_blocks)
    per_unit_ref[0] = start
    per_unit_ref[1] = start + tiles
    per_unit_ref[2] = jnp.where(n_lanes > 1.5, 0.5, 1.0)
    per_unit_ref[3] = n_lanes
    per_unit_ref[4] = eighth * 65536.0 + lane16 * 256.0 + 2.0 * unit + (1.0 - turned) - dummy
    spot = (iota((8, 128), 0) * 128 + iota((8, 128), 1)).astype(f32)
    n_full = -(-units * 64 // 1024)
    codes = [jnp.full((8, 128), dummy, f32) for _ in range(n_full)]
    for u in range(units):
        first, end, inverse, lanes, base = (jnp.broadcast_to(per_unit_ref[k, u : u + 1, :], (8, 128)) for k in range(5))
        for k in range(n_full):
            place = spot + 1024.0 * k
            at = place - first
            row = jnp.floor(at * inverse)
            code = base + row * 4096.0 + (at - row * lanes) * n_blocks
            code = code + jnp.where(row > 15.5, (groups - 1) * 65536.0, 0.0)
            codes[k] = codes[k] + jnp.where((at >= 0.0) & (place < end), code, 0.0)
    for k in range(n_full):
        list_ref[8 * k : 8 * k + 8, :] = codes[k].astype(i32)
    total = jnp.broadcast_to(jnp.sum(tiles, axis=0, keepdims=True), (8, 128))
    list_ref[8 * n_full : 8 * n_full + 8, :] = jnp.where(iota((8, 128), 0) == 0, dummy, total).astype(i32)
    copy = pltpu.make_async_copy(list_ref, list_smem, sem)
    copy.start()

    at = iota((8, 128), 0)
    eye = sum(jnp.where((at & 3) == c, v, 0.0) for c, v in enumerate(viewer))

    for n in range(n_blocks):
        raw = blocks_ref[n]
        moved = (raw + eye) * scale
        moved = moved * moved
        norm = 2.0 * (moved + pltpu.roll(moved, 7, 0) + pltpu.roll(moved, 6, 0))
        for h in range(2):
            xyz = raw * scale if h == 0 else pltpu.roll(raw * scale, 4, 0)
            weight = pltpu.roll(raw, 1 if h == 0 else 5, 0)
            norms = pltpu.roll(norm, 3 if h == 0 else 7, 0)
            rows_ref[h * n_blocks + n] = jnp.where(at < 3, xyz, jnp.where(at == 3, norms, weight))
    far = 2.0 * sum((v * scale) ** 2 for v in viewer)
    rows_ref[2 * n_blocks] = jnp.where(at == 3, jnp.float32(far), jnp.float32(0.0))
    for k in range(2 * groups):
        cols_ref[k * 128 : (k + 1) * 128, :] = rows_ref[pl.ds(k * 16, 16)].reshape(128, 128).T
    acc_ref[...] = jnp.zeros_like(acc_ref)
    copy.wait()
    trips = (list_smem[8 * n_full + 1, 0] + TILES - 1) // TILES

    def fill(trip):
        for t in range(TILES):
            place = trip * TILES + t
            code = list_smem[place >> 7, place & 127]
            start = pl.multiple_of((code >> 12) * 8, 8)
            terms = tile_terms(cols_ref[pl.ds(start, 8), :], ((code >> 8) & 15) * 8, rows_ref[code & 255])
            for k, v in enumerate(terms):
                terms_ref[t, k] = v

    def both_hats(t):
        s_at, s_part, mu_at, lower, upper = (terms_ref[t, k] for k in range(5))
        return hats(s_at, 1.0 - s_part, s_part, HS), hats(mu_at, lower, upper, HM)

    fill(0)

    def body(trip, carry):
        total = None
        for p in range(TILES // 2):
            s0, m0 = both_hats(2 * p)
            s1, m1 = both_hats(2 * p + 1)
            s = jnp.concatenate([jnp.concatenate(s0, 0), jnp.concatenate(s1, 0)], 1)
            m = jnp.concatenate([jnp.concatenate(m0, 0), jnp.concatenate(m1, 0)], 1)
            r = lax.dot_general(s, m, (((1,), (1,)), ((), ())), preferred_element_type=f32)
            total = r if total is None else total + r
        fill(trip + 1)
        acc_ref[...] += total
        return carry

    lax.fori_loop(0, trips, body, 0)

    sm = (8, 16 * HM)
    same = iota(sm, 0) == (iota(sm, 1) & 7)
    sums = []
    for k in range(SBINS):
        place = 16 * (k % HS) + 8 * (k // HS)
        sums.append(jnp.sum(jnp.where(same, acc_ref[place : place + 8, :], 0.0), axis=0, keepdims=True))
    by_s = jnp.concatenate(sums + [jnp.zeros((128 - SBINS, 16 * HM), f32)], axis=0)
    r, c = iota((32, 16 * HM), 0), iota((32, 16 * HM), 1)
    to_m = jnp.where((c >> 4) + HM * ((c >> 3) & 1) == r, 1.0, 0.0)
    bins = lax.dot_general(
        to_m, by_s, (((1,), (1,)), ((), ())), precision=lax.Precision.HIGHEST, preferred_element_type=f32
    )
    packed = bins[0:8]
    for k in range(1, 3):
        packed = packed + pltpu.roll(bins[8 * k : 8 * k + 8], 32 * k, 1)
    out_ref[...] = packed


def pair_counts(blocks):
    units = blocks.shape[0] // 2
    n_list = 8 * (-(-units * 64 // 1024) + 1)
    return pl.pallas_call(
        functools.partial(count_kernel, units),
        out_shape=pltpu.VMEM((8, 128), f32),
        in_specs=[pl.BlockSpec(memory_space=pltpu.VMEM)],
        out_specs=pl.BlockSpec(memory_space=pltpu.VMEM),
        scratch_shapes=[
            pltpu.VMEM((4 * units + 1, 8, 128), f32),
            pltpu.VMEM((2 * (units // 8) * 128, 128), f32),
            pltpu.VMEM((5, units, 128), f32),
            pltpu.VMEM((n_list, 128), i32),
            pltpu.SMEM((n_list, 128), i32),
            pltpu.VMEM((TILES, 5, 8, 128), f32),
            pltpu.VMEM((16 * HS, 16 * HM), f32),
            pltpu.SemaphoreType.DMA,
        ],
    )(blocks)


def in_vmem(x):
    return pltpu.with_memory_space_constraint(x, pltpu.VMEM)


def solution(mesh):
    n_gx, n_wa = mesh.shape["gx"], mesh.shape["wa"]
    units = 2 * n_wa
    scale = 10.0 * SBINS * MUBINS / (n_wa * units * 256 * 256)

    def per_device(positions, weights, block_count, send_list, unit_pair, unit_live):
        dealt = dealt_blocks(
            n_gx, n_wa, jnp.transpose(positions, (1, 0, 2)), weights, block_count,
            jnp.transpose(send_list, (0, 2, 1)), unit_pair, unit_live,
        )
        packed = pair_counts(in_vmem(dealt))
        slab, whole = totals(n_gx, n_wa, scale, in_vmem(packed))
        slab, whole = unpacked(in_vmem(slab), in_vmem(whole))
        return jnp.transpose(slab, (1, 2, 0)), whole.T

    return jax.shard_map(
        per_device,
        mesh=mesh,
        in_specs=(P(("gx", "wa")),) * 6,
        out_specs=(P("gx", None, None), P()),
        check_vma=False,
    )
```

profile of v0, /device:TPU:1, one launch (start us, length us, event | category | flops | bytes accessed | tf_op | source)
XLA Modules:
  0.0 46.4 jit_solution(18166218064873698784)
XLA Ops:
  1.3 19.4 %shard_map.77.blocks_ref = f32[64,8,128]{2,1,0:T(8,128)S(1)} custom-call(s32[1]{0:T(128)S(6)} %copy.8.live_ref, s32[16]{0:T(128)} %count_hbm.1, s32[1,2,16]{2,1,0:T(2,128)} %bitcast.5, s32[1,32]{1,0:T(1,128)} %pair_hbm.1, f32[3,16,256]{2,1,0:T(8,128)} %bitcast.4, f32[16,256]{1,0:T(8,128)} %wgt_hbm.1), custom_call_target="tpu_custom_call" | custom-call | tf_op jit(solution)/shard_map/pallas_call | solution.py:182
  20.7 7.9 %shard_map.78.in_ref = f32[8,128]{1,0:T(8,128)S(1)} custom-call(f32[64,8,128]{2,1,0:T(8,128)S(1)} %shard_map.77.blocks_ref), custom_call_target="tpu_custom_call" | custom-call | tf_op jit(solution)/shard_map/pallas_call | solution.py:398
  28.6 17.1 %shard_map.79 = (f32[8,128]{1,0:T(8,128)S(1)}, f32[8,128]{1,0:T(8,128)S(1)}) custom-call(f32[8,128]{1,0:T(8,128)S(1)} %shard_map.78.in_ref), custom_call_target="tpu_custom_call" | custom-call | tf_op jit(solution)/shard_map/pallas_call | solution.py:248
  45.7 0.7 %shard_map.80 = (f32[20,1,30]{2,1,0:T(1,128)}, f32[20,30]{1,0:T(8,128)}) custom-call(f32[8,128]{1,0:T(8,128)S(1)} %get-tuple-element.6.slab_ref, f32[8,128]{1,0:T(8,128)S(1)} %get-tuple-element.7.whole_ref), custom_call_target="tpu_custom_call" | custom-call | tf_op jit(solution)/shard_map/pallas_call | solution.py:276
where the time goes:
time: 46.6 us; the launch traced here: 46.4 us
  Pallas kernels  45.1 us (97%)
  between operations  1.3 us (3%)
    pallas_call x1, Pallas kernels, dealt_blocks(): pl.pallas_call(functools.partial(exchange_kernel, n_gx, n_wa), out_shape=...  19.4 us
    pallas_call x1, Pallas kernels, totals(): pl.pallas_call(functools.partial(total_kernel, n_gx, n_wa, scale), out_sh...  17.1 us
    pallas_call x1, Pallas kernels, pair_counts(): pl.pallas_call(functools.partial(count_kernel, units), out_shape=pltpu.VM...  7.93 us

commit v1 on v0

--- a/solution.py
+++ b/solution.py
@@ -139,15 +139,12 @@
     )[2]
     unit = iota((units, 128), 0).astype(f32)
     key = tiles * units + (units - 1 - unit)
-    on_lanes = jnp.sum(jnp.where(iota((units, 128), 0) == iota((units, 128), 1), key, 0.0), axis=0, keepdims=True)
-    more = (on_lanes > key) & (iota((units, 128), 1) < units)
-    rank = jnp.sum(jnp.where(more, 1.0, 0.0), axis=1, keepdims=True)
+    wide = (units, 8 * units)
+    key = jnp.concatenate([key] * -(-8 * units // 128), axis=1)[:, : 8 * units]
+    on_lanes = jnp.sum(jnp.where(iota(wide, 0) == (iota(wide, 1) >> 3), key, 0.0), axis=0, keepdims=True)
+    rank = jnp.sum(jnp.where(key > on_lanes, 1.0, 0.0), axis=0, keepdims=True)
     place = jnp.where(rank < n_wa, rank, (units - 1 + n_wa) - rank)
-    wide = (units, 8 * units)
-    target = jnp.sum(
-        jnp.where(iota(wide, 0) == (iota(wide, 1) >> 3), 8.0 * place + (iota(wide, 1) & 7).astype(f32), 0.0),
-        axis=0, keepdims=True,
-    )
+    target = 8.0 * place + (iota((1, 8 * units), 1) & 7).astype(f32)
     square = (8 * units, 8 * units)
     choice = jnp.where(iota(square, 0).astype(f32) == target, 1.0, 0.0).astype(bf16)
     left = jnp.concatenate([mine, partner], axis=1)
@@ -210,10 +207,10 @@
     barrier = pltpu.get_barrier_semaphore()
     wa_peers = [lax.rem(w + o, n_wa) for o in range(1, n_wa)]
     gx_peers = [lax.rem(g + o, n_gx) for o in range(1, n_gx)]
+    for p in gx_peers:
+        pl.semaphore_signal(barrier, inc=1, device_id=(p, w), device_id_type=MESH)
     for p in wa_peers:
         pl.semaphore_signal(barrier, inc=1, device_id=(g, p), device_id_type=MESH)
-    for p in gx_peers:
-        pl.semaphore_signal(barrier, inc=1, device_id=(p, w), device_id_type=MESH)
     pl.semaphore_wait(barrier, n_wa + n_gx - 2)
 
     for p in gx_peers:
@@ -293,8 +290,11 @@
         return [blocks_ref[pl.ds(s, units, stride=2), 4 * h + 3, :] for h in range(2)]
 
     turned, n_lanes, tiles = plan(weights_of(0), weights_of(1))
-    low = iota((units, units), 1) < iota((units, units), 0)
-    start = jnp.dot(jnp.where(low, 1.0, 0.0), tiles, preferred_element_type=f32)
+    start, step = tiles, 1
+    while step < units:
+        start = start + jnp.where(iota((units, 128), 0) >= step, pltpu.roll(start, step, 0), 0.0)
+        step *= 2
+    start = start - tiles
     unit = iota((units, 128), 0).astype(f32)
     eighth = jnp.floor(unit / 8)
     lane16 = 2.0 * (unit - 8.0 * eighth) + turned
@@ -326,20 +326,30 @@
     at = iota((8, 128), 0)
     eye = sum(jnp.where((at & 3) == c, v, 0.0) for c, v in enumerate(viewer))
 
-    for n in range(n_blocks):
-        raw = blocks_ref[n]
-        moved = (raw + eye) * scale
-        moved = moved * moved
-        norm = 2.0 * (moved + pltpu.roll(moved, 7, 0) + pltpu.roll(moved, 6, 0))
+    share = max(1, groups // 2)
+
+    def prepare(turn, carry):
+        for i in range(16 * share):
+            n = turn * (16 * share) + i
+            raw = blocks_ref[n]
+            moved = (raw + eye) * scale
+            moved = moved * moved
+            norm = 2.0 * (moved + pltpu.roll(moved, 7, 0) + pltpu.roll(moved, 6, 0))
+            for h in range(2):
+                xyz = raw * scale if h == 0 else pltpu.roll(raw * scale, 4, 0)
+                weight = pltpu.roll(raw, 1 if h == 0 else 5, 0)
+                norms = pltpu.roll(norm, 3 if h == 0 else 7, 0)
+                rows_ref[h * n_blocks + n] = jnp.where(at < 3, xyz, jnp.where(at == 3, norms, weight))
         for h in range(2):
-            xyz = raw * scale if h == 0 else pltpu.roll(raw * scale, 4, 0)
-            weight = pltpu.roll(raw, 1 if h == 0 else 5, 0)
-            norms = pltpu.roll(norm, 3 if h == 0 else 7, 0)
-            rows_ref[h * n_blocks + n] = jnp.where(at < 3, xyz, jnp.where(at == 3, norms, weight))
+            for k in range(share):
+                group = h * groups + turn * share + k
+                place = pl.multiple_of(group * 128, 128)
+                cols_ref[pl.ds(place, 128), :] = rows_ref[pl.ds(group * 16, 16)].reshape(128, 128).T
+        return carry
+
+    lax.fori_loop(0, groups // share, prepare, 0)
     far = 2.0 * sum((v * scale) ** 2 for v in viewer)
     rows_ref[2 * n_blocks] = jnp.where(at == 3, jnp.float32(far), jnp.float32(0.0))
-    for k in range(2 * groups):
-        cols_ref[k * 128 : (k + 1) * 128, :] = rows_ref[pl.ds(k * 16, 16)].reshape(128, 128).T
     acc_ref[...] = jnp.zeros_like(acc_ref)
     copy.wait()
     trips = (list_smem[8 * n_full + 1, 0] + TILES - 1) // TILES

time: 46.6 us -> 45 us (0.966)
  Pallas kernels: 45.1 us -> 43.1 us
    pallas_call x1, Pallas kernels: 17.1 us -> 12.5 us  [totals(): pl.pallas_call(functools.partial(total_kernel, n_gx, n_wa, scale), out_sh...]
    pallas_call x1, Pallas kernels: 7.93 us -> 10.7 us  [pair_counts(): pl.pallas_call(functools.partial(count_kernel, units), out_shape=pltpu.VM...]
where the time goes in v1:
time: 45 us; the launch traced here: 44.4 us
  Pallas kernels  43.1 us (96%)
  between operations  1.3 us (3%)
    pallas_call x1, Pallas kernels, dealt_blocks(): pl.pallas_call(functools.partial(exchange_kernel, n_gx, n_wa), out_shape=...  19.3 us
    pallas_call x1, Pallas kernels, totals(): pl.pallas_call(functools.partial(total_kernel, n_gx, n_wa, scale), out_sh...  12.5 us
    pallas_call x1, Pallas kernels, pair_counts(): pl.pallas_call(functools.partial(count_kernel, units), out_shape=pltpu.VM...  10.7 us

profile of v1, /device:TPU:1, one launch (start us, length us, event | category | flops | bytes accessed | tf_op | source)
XLA Modules:
  0.0 44.4 jit_solution(6890955625581331080)
XLA Ops:
  1.3 19.3 %shard_map.77.blocks_ref = f32[64,8,128]{2,1,0:T(8,128)S(1)} custom-call(s32[1]{0:T(128)S(6)} %copy.8.live_ref, s32[16]{0:T(128)} %count_hbm.1, s32[1,2,16]{2,1,0:T(2,128)} %bitcast.5, s32[1,32]{1,0:T(1,128)} %pair_hbm.1, f32[3,16,256]{2,1,0:T(8,128)} %bitcast.4, f32[16,256]{1,0:T(8,128)} %wgt_hbm.1), custom_call_target="tpu_custom_call" | custom-call | tf_op jit(solution)/shard_map/pallas_call | solution.py:179
  20.6 10.7 %shard_map.78.in_ref = f32[8,128]{1,0:T(8,128)S(1)} custom-call(f32[64,8,128]{2,1,0:T(8,128)S(1)} %shard_map.77.blocks_ref), custom_call_target="tpu_custom_call" | custom-call | tf_op jit(solution)/shard_map/pallas_call | solution.py:408
  31.3 12.5 %shard_map.79 = (f32[8,128]{1,0:T(8,128)S(1)}, f32[8,128]{1,0:T(8,128)S(1)}) custom-call(f32[8,128]{1,0:T(8,128)S(1)} %shard_map.78.in_ref), custom_call_target="tpu_custom_call" | custom-call | tf_op jit(solution)/shard_map/pallas_call | solution.py:245
  43.8 0.7 %shard_map.80 = (f32[20,1,30]{2,1,0:T(1,128)}, f32[20,30]{1,0:T(8,128)}) custom-call(f32[8,128]{1,0:T(8,128)S(1)} %get-tuple-element.6.slab_ref, f32[8,128]{1,0:T(8,128)S(1)} %get-tuple-element.7.whole_ref), custom_call_target="tpu_custom_call" | custom-call | tf_op jit(solution)/shard_map/pallas_call | solution.py:273
